TPU v7x, 128 devices: a 2x2x16 block of a 8x8x16 slice. The times are simulated.
128 devices in a mesh: groups: 4 (over x, y), blk: 32 (over z, core).
Axes of the slice: x: 2, y: 2, z: 16, core: 2. Of those that a mesh axis runs over, the one named last changes fastest.
The devices are a block of a 8x8x16 slice.
Arguments:
- points: bfloat16 [196608, 1024], P(('groups', 'blk')), parts along dimension 0, may hold values from -6 to 6
- coverage: float32 [196608], P(('groups', 'blk')), parts along dimension 0, may hold values from 0 to 1.5
- candidates: bfloat16 [16384, 1024], P(('groups', 'blk')), parts along dimension 0, may hold values from -6 to 6
- cand_count: int32 [128], P(('groups', 'blk')), parts along dimension 0, may hold values from 16 to 128, as said below
- acc_index: int32 [128, 16], P(('groups', 'blk')), parts along dimension 0, may hold values from 0 to 127, as said below
Outputs:
- gain_out: float32 [16384], P(('groups', 'blk')), parts along dimension 0
- new_coverage: float32 [196608], P(('groups', 'blk')), parts along dimension 0
There are 4 independent parts, one for each index of `groups`. A program takes and returns all parts, laid end to end along the dimension named above; each array names one. Nothing has to cross between parts.
Inputs may be any that keep to these rules, and one draw needn't show every extreme that they name: `cand_count`: some device has all 128 slots live. `acc_index`: each entry of row b is below cand_count[b]; entries may repeat.
All inputs are finite; a program needn't handle non-finite values.
Results may differ from a plain program's by a relative error of at most 0.0003.
Values may be sent and summed in bfloat16 or wider, within the bound.
A program may use at most 64 MiB of HBM per device.

v0:
```python
import jax
import jax.numpy as jnp
from jax import lax
from jax.sharding import Mesh
from jax.sharding import PartitionSpec as P

BLK = ("blk_0", "blk_1")
GROUPS_BLK = ("groups", "blk_0", "blk_1")


def in_blocks(shard, dim, count):
    dims = shard.shape
    parts = shard.reshape(*dims[:dim], count, dims[dim] // count, *dims[dim + 1 :])
    return jnp.moveaxis(parts, dim, 0)


def summed_on_arrival(shard, axis, dim):
    parts = in_blocks(shard, dim, lax.axis_size(axis))
    arrived = lax.all_to_all(parts, axis, split_axis=0, concat_axis=0, tiled=True)
    return arrived.sum(axis=0)


def gathered_by_axis(shard, axes, dim):
    if not axes:
        return shard
    nearer = lax.all_gather(shard, axes[-1], axis=dim, tiled=True)
    return gathered_by_axis(nearer, axes[:-1], dim)


def block_terms(points, coverage, cand_block, factor):
    similar = (
        jnp.einsum("pd,cd->pc", points, cand_block, preferred_element_type=jnp.float32) * factor
    )
    return (similar, jnp.sum(jnp.maximum(similar - coverage[:, None], 0.0), axis=0))


def per_device(points, coverage, candidates, cand_count, acc_index):
    width = points.shape[1]
    slots = candidates.shape[0]
    factor = 1.0 / jnp.sqrt(jnp.float32(width))
    devices = lax.axis_size(BLK)
    point_total = jnp.float32(points.shape[0] * devices)
    slot_ids = jnp.arange(slots, dtype=jnp.int32)
    cover = coverage
    shard_rows = lax.all_gather(candidates, BLK, axis=0, tiled=True)
    similar, sums = block_terms(points, coverage, shard_rows, factor)
    every_sum = sums
    every_sum, cover = (every_sum, cover)
    gain_sum = summed_on_arrival(every_sum, BLK, 0)
    live_rows = slot_ids < cand_count[0]
    gain_out = jnp.where(live_rows, gain_sum / point_total, 0.0)
    picked = jnp.take(candidates, acc_index[0], axis=0)
    similar = (
        jnp.einsum(
            "pd,ad->pa",
            points,
            gathered_by_axis(picked, ("blk_1", "blk_0"), 0),
            preferred_element_type=jnp.float32,
        )
        * factor
    )
    new_coverage = jnp.maximum(coverage, jnp.max(similar, axis=1))
    return (gain_out, new_coverage)


def solution(mesh):
    split = Mesh(mesh.devices.reshape(mesh.shape["groups"], 16, 2), ("groups", "blk_0", "blk_1"))
    return jax.shard_map(
        per_device,
        mesh=split,
        in_specs=(
            P(GROUPS_BLK, None),
            P(GROUPS_BLK),
            P(GROUPS_BLK, None),
            P(GROUPS_BLK),
            P(GROUPS_BLK, None),
        ),
        out_specs=(P(GROUPS_BLK), P(GROUPS_BLK)),
        check_vma=False,
    )
```

profile of v0, /device:TPU:84, one launch (start us, length us, event | category | flops | bytes accessed | tf_op | source)
XLA Modules:
  0.0 137.2 jit_solution(8278887492679083085)
XLA Ops:
  7.2 0.0 copy-start
  7.2 0.1 all-gather.3.cloned.1.call-start
  7.3 0.7 all-gather.3.cloned.1.call-update
  8.0 0.1 all-gather.5.cloned.1.call-start
  8.1 0.7 fusion.1
  8.8 1.6 %gather_fusion = bf16[16,1024]{1,0:T(8,128)(2,1)S(1)} fusion(bf16[128,1024]{1,0:T(8,128)(2,1)} %param.7, s32[1024]{0:T(1024)S(1)} %pad_clamp_fusion), kind=kCustom, calls=%fused_computation | custom fusion | bytes 65600 | tf_op jit(solution)/shard_map/jit(_take)/gather | solution.py:52
  10.4 0.7 compare_and_fusion
  11.1 0.1 broadcast_select_fusion
  11.1 46.4 %all_gather.10 = bf16[256,1024]{1,0:T(8,128)(2,1)} all-gather(bf16[16,1024]{1,0:T(8,128)(2,1)S(1)} %broadcast_select_fusion), channel_id=1, replica_groups=mesh['groups'=4,'blk_0'=16,'blk_1'=2] {'blk_0'}, dimensions={0}, use_global_device_ids=true | all-gather | bytes 557056 | tf_op jit(solution)/shard_map/all_gather | solution.py:26
  57.5 0.1 all-gather.5.cloned.1.call-update
  58.2 34.8 %all-gather.3.cloned.1.call-done = bf16[4096,1024]{1,0:T(8,128)(2,1)} async-done(((bf16[128,1024]{1,0:T(8,128)(2,1)}), bf16[4096,1024]{1,0:T(8,128)(2,1)}) %all-gather.3.cloned.1.call-update) | async-done | bytes 8388624 | tf_op jit(solution)/shard_map/all_gather | solution.py:45
  93.0 0.0 copy-done
  93.0 17.1 %maximum_reduce_fusion = f32[4096]{0:T(1024)} fusion(bf16[1536,1024]{1,0:T(8,128)(2,1)S(1)} %copy-done, bf16[4096,1024]{1,0:T(8,128)(2,1)} %all-gather.3.cloned.1.call-done, f32[1536]{0:T(1024)} %param.6), kind=kOutput, calls=%fused_computation.1 | convolution fusion | flops 12910063616 | bytes 11556864 | tf_op jit(solution)/shard_map/pd,cd->pc/dot_general | solution.py:32
  110.2 0.0 copy-start.1
  110.2 7.9 %all-to-all-start = ((f32[32,1,128]{2,1,0:T(1,128)}), f32[32,1,128]{2,1,0:T(1,128)S(1)}, u32[]{:S(2)}, u32[]{:S(2)}) async-start(f32[32,1,128]{2,1,0:T(1,128)} %bitcast.1), calls=%async_computation | async-start | bytes 32768 | tf_op jit(solution)/shard_map/all_to_all | solution.py:19
  118.0 0.0 all-gather.5.cloned.1.call-done
  118.1 3.1 %fusion = f32[1536]{0:T(1024)S(1)} fusion(bf16[512,1024]{1,0:T(8,128)(2,1)} %all-gather.5.cloned.1.call-done, bf16[1536,1024]{1,0:T(8,128)(2,1)S(1)} %copy-done), kind=kOutput, calls=%fused_computation.3 | convolution fusion | flops 1612184064 | bytes 4200448 | tf_op jit(solution)/shard_map/pd,ad->pa/dot_general | solution.py:54
  121.1 0.0 copy-done.1
  121.2 0.6 max.11
  121.8 8.1 %all-to-all-done = f32[32,1,128]{2,1,0:T(1,128)S(1)} async-done(((f32[32,1,128]{2,1,0:T(1,128)}), f32[32,1,128]{2,1,0:T(1,128)S(1)}, u32[]{:S(2)}, u32[]{:S(2)}) %all-to-all-start) | async-done | bytes 16416 | tf_op jit(solution)/shard_map/all_to_all | solution.py:19
  129.9 0.5 compare_select_fusion.2
  (2 shorter events, 0.0 us)
Async XLA Ops:
  7.2 85.9 %copy-start = (bf16[1536,1024]{1,0:T(8,128)(2,1)S(1)}, bf16[1536,1024]{1,0:T(8,128)(2,1)}, u32[]{:S(2)}) copy-start(bf16[1536,1024]{1,0:T(8,128)(2,1)} %param.5) | copy-start | bytes 9437188
  7.2 85.8 %all-gather.3.cloned.1.call-start = ((), (), s32[]{:S(2)}) async-start(), calls=%async_computation.1 | async-start | bytes 8650752 | tf_op jit(solution)/shard_map/all_gather | solution.py:45
  8.0 110.1 %all-gather.5.cloned.1.call-start = ((), (), s32[]{:S(2)}) async-start(), calls=%async_computation.2 | async-start | bytes 1572864 | tf_op jit(solution)/shard_map/all_gather | solution.py:26
  110.2 11.0 %copy-start.1 = (f32[1536]{0:T(1024)S(1)}, f32[1536]{0:T(1024)}, u32[]{:S(2)}) copy-start(f32[1536]{0:T(1024)} %param.6) | copy-start | bytes 18436
  110.2 19.7 %all-to-all-start = ((f32[32,1,128]{2,1,0:T(1,128)}), f32[32,1,128]{2,1,0:T(1,128)S(1)}, u32[]{:S(2)}, u32[]{:S(2)}) async-start(f32[32,1,128]{2,1,0:T(1,128)} %bitcast.1), calls=%async_computation | async-start | bytes 32768 | tf_op jit(solution)/shard_map/all_to_all | solution.py:19
Sparse Core Ops, SparseCore 0:
  9.7 83.2 all-gather.2
  94.7 11.6 all-gather.4
where the time goes:
time: 138 us; the launch traced here: 137 us
  blocking collectives  46.4 us (34%)
  waiting for transfers between devices  43.7 us (32%)
  matrix products  20.2 us (15%)
  between operations  14.8 us (11%)
  starting transfers between devices  8 us (6%)
  other arithmetic  2.62 us (2%)
  local copies, waits for them, and re-layouts  1.61 us (1%)
    all_gather x1, blocking collectives, gathered_by_axis(): nearer = lax.all_gather(shard, axes[-1], axis=dim, tiled=True)  46.4 us
    all_gather x1, waiting for transfers between devices, per_device(): shard_rows = lax.all_gather(candidates, BLK, axis=0, tiled=True)  34.8 us
    dot_general x1, matrix products, block_terms(): jnp.einsum('pd,cd->pc', points, cand_block, preferred_element_type=jnp.fl...  17.1 us
    all_to_all x1, waiting for transfers between devices, summed_on_arrival(): lax.all_to_all(parts, axis, split_axis=0, concat_axis=0, tiled=True)  8.09 us
    all_to_all x1, starting transfers between devices, summed_on_arrival(): lax.all_to_all(parts, axis, split_axis=0, concat_axis=0, tiled=True)  7.88 us
    dot_general x1, matrix products, per_device(): jnp.einsum('pd,ad->pa', points, gathered_by_axis(picked, ('blk_1', 'blk_0...  3.06 us
  transfers between devices with their start and end apart: 3, of which 2 were waited for; matrix products, arithmetic and copies ran while one was open for 17% of the time, Pallas kernels for 0%

commit v1 on v0

--- a/solution.py
+++ b/solution.py
@@ -42,7 +42,9 @@
     point_total = jnp.float32(points.shape[0] * devices)
     slot_ids = jnp.arange(slots, dtype=jnp.int32)
     cover = coverage
-    shard_rows = lax.all_gather(candidates, BLK, axis=0, tiled=True)
+    shard_rows = jnp.concatenate(
+        lax.all_to_all(jnp.stack([candidates] * lax.axis_size(BLK)), BLK, 0, 0), axis=0
+    )
     similar, sums = block_terms(points, coverage, shard_rows, factor)
     every_sum = sums
     every_sum, cover = (every_sum, cover)

time: 138 us -> 470 us (3.41)
  blocking collectives: 46.4 us -> 390 us
  waiting for transfers between devices: 43.7 us -> 8.17 us
  starting transfers between devices: 8 us -> 29.3 us
    all_gather x1, blocking collectives: 46.4 us -> 390 us  [gathered_by_axis(): nearer = lax.all_gather(shard, axes[-1], axis=dim, tiled=True)]
    all_gather x1 -> x0, waiting for transfers between devices: 34.8 us -> none  [per_device(): shard_rows = lax.all_gather(candidates, BLK, axis=0, tiled=True)]
    all_to_all x0 -> x1, starting transfers between devices: none -> 17.9 us  [per_device(): lax.all_to_all(jnp.stack([candidates] * lax.axis_size(BLK)), BLK, 0, 0)]
    another operation x0 -> x1, local copies, waits for them, and re-layouts: none -> 5.4 us  [per_device(): jnp.stack([candidates] * lax.axis_size(BLK))]
  transfers between devices with their start and end apart: 3 -> 3, of which waited for: 2 -> 1; matrix products, arithmetic and copies ran while one was open for 17% -> 5% of each run, Pallas kernels for 0% -> 0%
where the time goes in v1:
time: 470 us
  blocking collectives  390 us (83%)
  starting transfers between devices  29.3 us (6%)
  matrix products  20.2 us (4%)
  between operations  14.8 us (3%)
  waiting for transfers between devices  8.17 us (2%)
  local copies, waits for them, and re-layouts  6.01 us (1%)
    all_gather x1, blocking collectives, gathered_by_axis(): nearer = lax.all_gather(shard, axes[-1], axis=dim, tiled=True)  390 us
    all_to_all x1, starting transfers between devices, per_device(): lax.all_to_all(jnp.stack([candidates] * lax.axis_size(BLK)), BLK, 0, 0)  17.9 us
    dot_general x1, matrix products, block_terms(): jnp.einsum('pd,cd->pc', points, cand_block, preferred_element_type=jnp.fl...  17.2 us
    all_to_all x1, starting transfers between devices, summed_on_arrival(): lax.all_to_all(parts, axis, split_axis=0, concat_axis=0, tiled=True)  11.3 us
  transfers between devices with their start and end apart: 3, of which 1 were waited for; matrix products, arithmetic and copies ran while one was open for 5% of the time, Pallas kernels for 0%

profile of v1, /device:TPU:84, one launch (start us, length us, event | category | flops | bytes accessed | tf_op | source)
XLA Modules:
  0.0 469.6 jit_solution(15381116500284938201)
XLA Ops:
  7.2 0.0 copy-start
  7.2 5.4 %stack.2 = bf16[32,128,1024]{2,1,0:T(8,128)(2,1)} broadcast(bf16[128,1024]{1,0:T(8,128)(2,1)} %param.7), dimensions={1,2} | broadcast | bytes 8650752 | tf_op jit(solution)/shard_map/stack | solution.py:46
  12.6 0.0 copy-start.3
  12.6 0.0 copy-start.1
  12.6 0.0 copy-start.2
  12.6 17.9 %all-to-all-start = ((bf16[32,128,1024]{2,1,0:T(8,128)(2,1)}), bf16[32,128,1024]{2,1,0:T(8,128)(2,1)}, u32[]{:S(2)}, u32[]{:S(2)}) async-start(bf16[32,128,1024]{2,1,0:T(8,128)(2,1)} %stack.2), calls=%async_computation | async-start | bytes 16777216 | tf_op jit(solution)/shard_map/all_to_all | solution.py:46
  30.6 0.1 all-gather.2.cloned.1.call-start
  30.6 0.0 copy-done.3
  30.7 0.0 copy-done.1
  30.7 0.6 gather_fusion
  31.3 0.1 broadcast_select_fusion
  31.4 389.8 %all_gather.6 = bf16[256,1024]{1,0:T(8,128)(2,1)} all-gather(bf16[16,1024]{1,0:T(8,128)(2,1)S(1)} %broadcast_select_fusion), channel_id=1, replica_groups=mesh['groups'=4,'blk_0'=16,'blk_1'=2] {'blk_0'}, dimensions={0}, use_global_device_ids=true | all-gather | bytes 557056 | tf_op jit(solution)/shard_map/all_gather | solution.py:26
  421.2 0.1 all-gather.2.cloned.1.call-update
  421.9 0.0 all-to-all-done
  421.9 0.0 copy-done
  421.9 0.0 copy-done.2
  421.9 17.2 %maximum_reduce_fusion = f32[4096]{0:T(1024)} fusion(bf16[1536,1024]{1,0:T(8,128)(2,1)S(1)} %copy-done, bf16[4096,1024]{1,0:T(8,128)(2,1)} %bitcast.1, f32[1536]{0:T(1024)S(1)} %copy-done.2), kind=kOutput, calls=%fused_computation.1 | convolution fusion | flops 12910063616 | bytes 11556864 | tf_op jit(solution)/shard_map/pd,cd->pc/dot_general | solution.py:32
  439.1 11.3 %all-to-all-start.1 = ((f32[32,1,128]{2,1,0:T(1,128)}), f32[32,1,128]{2,1,0:T(1,128)S(1)}, u32[]{:S(2)}, u32[]{:S(2)}) async-start(f32[32,1,128]{2,1,0:T(1,128)} %bitcast.2), calls=%async_computation.1 | async-start | bytes 32768 | tf_op jit(solution)/shard_map/all_to_all | solution.py:19
  450.4 0.0 all-gather.2.cloned.1.call-done
  450.4 3.1 fusion
  453.5 0.6 max.11
  454.1 8.1 %all-to-all-done.1 = f32[32,1,128]{2,1,0:T(1,128)S(1)} async-done(((f32[32,1,128]{2,1,0:T(1,128)}), f32[32,1,128]{2,1,0:T(1,128)S(1)}, u32[]{:S(2)}, u32[]{:S(2)}) %all-to-all-start.1) | async-done | bytes 16416 | tf_op jit(solution)/shard_map/all_to_all | solution.py:19
  462.2 0.5 compare_select_fusion.2
  (4 shorter events, 0.0 us)
Async XLA Ops:
  7.2 414.7 %copy-start = (bf16[1536,1024]{1,0:T(8,128)(2,1)S(1)}, bf16[1536,1024]{1,0:T(8,128)(2,1)}, u32[]{:S(2)}) copy-start(bf16[1536,1024]{1,0:T(8,128)(2,1)} %param.5) | copy-start | bytes 9437188
  12.6 18.0 %copy-start.3 = (s32[1,16]{1,0:T(1,128)S(1)}, s32[1,16]{1,0:T(1,128)}, u32[]{:S(2)}) copy-start(s32[1,16]{1,0:T(1,128)} %param.9) | copy-start | bytes 196
  12.6 18.1 %copy-start.1 = (bf16[128,1024]{1,0:T(8,128)(2,1)S(1)}, bf16[128,1024]{1,0:T(8,128)(2,1)}, u32[]{:S(2)}) copy-start(bf16[128,1024]{1,0:T(8,128)(2,1)} %param.7) | copy-start | bytes 786436
  12.6 409.3 %copy-start.2 = (f32[1536]{0:T(1024)S(1)}, f32[1536]{0:T(1024)}, u32[]{:S(2)}) copy-start(f32[1536]{0:T(1024)} %param.6) | copy-start | bytes 18436
  12.6 409.3 %all-to-all-start = ((bf16[32,128,1024]{2,1,0:T(8,128)(2,1)}), bf16[32,128,1024]{2,1,0:T(8,128)(2,1)}, u32[]{:S(2)}, u32[]{:S(2)}) async-start(bf16[32,128,1024]{2,1,0:T(8,128)(2,1)} %stack.2), calls=%async_computation | async-start | bytes 16777216 | tf_op jit(solution)/shard_map/all_to_all | solution.py:46
  30.6 419.9 %all-gather.2.cloned.1.call-start = ((), (), s32[]{:S(2)}) async-start(), calls=%async_computation.2 | async-start | bytes 1572864 | tf_op jit(solution)/shard_map/all_gather | solution.py:26
  439.1 23.1 %all-to-all-start.1 = ((f32[32,1,128]{2,1,0:T(1,128)}), f32[32,1,128]{2,1,0:T(1,128)S(1)}, u32[]{:S(2)}, u32[]{:S(2)}) async-start(f32[32,1,128]{2,1,0:T(1,128)} %bitcast.2), calls=%async_computation.1 | async-start | bytes 32768 | tf_op jit(solution)/shard_map/all_to_all | solution.py:19
Sparse Core Ops, SparseCore 0:
  421.4 16.0 all-gather.1
